TPU v7x, 128 devices: a whole 4x4x4 slice. The times are simulated.
128 devices in a mesh: rep: 2 (over z_hi), shard: 64 (over y, z_lo, x, core).
Axes of the slice: x: 4, y: 4, z: 4 (z_hi: 2, z_lo: 2; z = z_hi * 2 + z_lo), core: 2. Of those that a mesh axis runs over, the one named last changes fastest.
Arguments:
- dense: bfloat16 [32768, 128], P(('rep', 'shard')), may hold values from -6 to 6
- small_ids: int32 [32768, 32], P(('rep', 'shard')), may hold values from 0 to 511
- labels: int32 [32768], P(('rep', 'shard')), may hold values 0 or 1
- small_tables: bfloat16 [32, 512, 128], replicated, may hold values from -6 to 6
- large_tables: bfloat16 [64, 8192, 128], P('shard'), may hold values from -6 to 6
- batch_sizes: int32 [64, 128], replicated, may hold values from 1 to 128, as said below
- bag_ends: int32 [64, 128, 128], P('shard'), may hold values from 0 to 256, as said below
- owner_row_index: int32 [64, 128, 256], P('shard'), may hold values from 0 to 8191
- w_first: bfloat16 [4784, 1024], replicated, may hold values from -0.09375 to 0.09375
- b_first: float32 [1024], replicated, may hold values from -3 to 3
- w_out: float32 [1024], replicated, may hold values from -0.1875 to 0.1875
Outputs:
- small_new: bfloat16 [32, 512, 128], replicated
- large_new: bfloat16 [64, 8192, 128], P('shard')
Inputs may be any that keep to these rules, and one draw needn't show every extreme that they name: `batch_sizes`: every feature has some owner, and every owner some feature, with exactly 128. `bag_ends`: nondecreasing along the last dimension; bags j >= batch_sizes[f, d] are empty; some bag list reaches 256.
All inputs are finite; a program needn't handle non-finite values. No bound on the sum of `labels` on one device may be relied on, other than what follows from the above.
Results may differ from a plain program's by a relative error of at most 0.0095.
Values may be sent and summed in bfloat16 or wider, within the bound.
A program may use at most 192 MiB of HBM per device.

v0:
```python
import jax
import jax.numpy as jnp
from jax import lax
from jax.sharding import PartitionSpec as P

step_size = 32.0


def as_sent(array):

    def short(part):
        return part.astype(jnp.bfloat16) if part.dtype == jnp.float32 else part

    return jax.tree.map(short, array)


def gathered_total(array, axis):
    return lax.all_gather(array, axis).astype(jnp.float32).sum(0)


def bag_members(limits, slot_total):
    starts = jnp.concatenate(
        [jnp.zeros(limits.shape[:-1] + (1,), jnp.int32), limits[..., :-1]], axis=-1
    )
    positions = jnp.arange(slot_total, dtype=jnp.int32)
    inside = (positions >= starts[..., None]) & (positions < limits[..., None])
    return inside.astype(jnp.bfloat16)


def silu_slope(preacts):
    squash = jax.nn.sigmoid(preacts)
    return squash * (1.0 + preacts * (1.0 - squash))


def spread_table(size_table, batch_rows, bag_span):
    chosen = jnp.arange(batch_rows, dtype=jnp.int32) * size_table[..., None] // batch_rows
    return (chosen[..., None] == jnp.arange(bag_span, dtype=jnp.int32)).astype(jnp.bfloat16)


def take_rows(table_one, row_list):
    return table_one[row_list]


def lower_pairs(gram_matrix, vec_count):
    pieces = [gram_matrix[:, index, :index] for index in range(1, vec_count)]
    return jnp.concatenate(pieces, axis=1)


def lower_square(pair_grad, vec_count):
    rows_list = []
    offset = 0
    for index in range(vec_count):
        piece = pair_grad[:, offset : offset + index]
        offset = offset + index
        rows_list.append(jnp.pad(piece, ((0, 0), (0, vec_count - index))))
    return jnp.stack(rows_list, axis=1)


def table_grads(row_list, members, gradient_list, row_total):
    slot_vectors = jnp.einsum(
        "fdks,fdke->fdse", members, gradient_list, preferred_element_type=jnp.float32
    )
    embed_width = gradient_list.shape[-1]

    def one_table(values, row_index):
        return jax.ops.segment_sum(
            values.reshape(-1, embed_width), row_index.reshape(-1), row_total
        )

    return jax.vmap(one_table)(slot_vectors, row_list)


def shards(
    dense,
    small_ids,
    labels,
    small_tables,
    large_tables,
    batch_sizes,
    bag_ends,
    owner_row_index,
    w_first,
    b_first,
    w_out,
):
    groups = lax.axis_size("shard")
    replica = lax.axis_index("rep")
    member_id = lax.axis_index("shard")
    batch_rows, embed_width = dense.shape
    owned_tables, embedding_rows = (large_tables.shape[0], large_tables.shape[1])
    small_count, small_rows = (small_tables.shape[0], small_tables.shape[1])
    feat_count = batch_sizes.shape[0]
    bag_span = bag_ends.shape[2]
    slot_total = owner_row_index.shape[2]
    pair_count = w_first.shape[0] - embed_width
    vec_count = 1 + small_count + feat_count
    first_dest = replica * groups
    own_limits = lax.dynamic_slice_in_dim(bag_ends, first_dest, groups, 1)
    own_rows = lax.dynamic_slice_in_dim(owner_row_index, first_dest, groups, 1)
    recv_sizes = lax.dynamic_slice_in_dim(batch_sizes, first_dest + member_id, 1, 1)[:, 0]
    members = bag_members(own_limits, slot_total)
    collected_rows = jax.vmap(take_rows)(large_tables, own_rows)
    pooled = jnp.einsum(
        "fdks,fdse->fdke", members, collected_rows, preferred_element_type=jnp.float32
    ).astype(jnp.bfloat16)
    arrived = lax.all_to_all(pooled, "shard", split_axis=1, concat_axis=0, tiled=True)
    recv_spread = spread_table(recv_sizes, batch_rows, bag_span)
    large_feat = jnp.einsum(
        "fbj,fje->bfe", recv_spread, arrived[:, 0], preferred_element_type=jnp.float32
    ).astype(jnp.bfloat16)
    small_hot = (small_ids[:, :, None] == jnp.arange(small_rows, dtype=jnp.int32)).astype(
        jnp.bfloat16
    )
    minor_feature = jnp.einsum(
        "btr,tre->bte", small_hot, small_tables, preferred_element_type=jnp.float32
    ).astype(jnp.bfloat16)
    vectors = jnp.concatenate([dense[:, None, :], minor_feature, large_feat], axis=1)
    gram_matrix = jnp.einsum("bie,bje->bij", vectors, vectors, preferred_element_type=jnp.float32)
    pair_values = (lower_pairs(gram_matrix, vec_count) * embed_width ** (-0.5)).astype(jnp.bfloat16)
    features = jnp.concatenate([pair_values, dense], axis=1)
    preact = jnp.dot(features, w_first, preferred_element_type=jnp.float32) + b_first
    hidden = jax.nn.silu(preact)
    logits = jnp.sum(hidden * w_out[None, :], axis=1)
    logit_grad = jax.nn.sigmoid(logits) - labels.astype(jnp.float32)
    pre_grad = (logit_grad[:, None] * w_out[None, :] * silu_slope(preact)).astype(jnp.bfloat16)
    pair_grad = jnp.einsum(
        "bh,ph->bp", pre_grad, w_first[:pair_count], preferred_element_type=jnp.float32
    ) * embed_width ** (-0.5)
    lower_part = lower_square(pair_grad, vec_count)
    symmetric = lower_part + jnp.swapaxes(lower_part, 1, 2)
    vec_grad = jnp.einsum("bij,bje->bie", symmetric, vectors.astype(jnp.float32)).astype(
        jnp.bfloat16
    )
    small_local = jnp.einsum(
        "btr,bte->tre",
        small_hot,
        vec_grad[:, 1 : 1 + small_count],
        preferred_element_type=jnp.float32,
    )
    small_sum = lax.psum(small_local, ("rep", "shard"))
    small_new = (small_tables.astype(jnp.float32) - step_size * small_sum).astype(jnp.bfloat16)
    large_grad_part = vec_grad[:, 1 + small_count :]
    folded = jnp.einsum(
        "fbj,bfe->fje", recv_spread, large_grad_part, preferred_element_type=jnp.float32
    ).astype(jnp.bfloat16)
    accumulate_gradient = lax.all_to_all(
        folded[:, None], "shard", split_axis=0, concat_axis=1, tiled=True
    )
    local_grad = table_grads(own_rows, members, accumulate_gradient, embedding_rows)
    large_grad = jax.tree.map(
        lambda part: part.astype(jnp.float32),
        jax.tree.map(lambda part: gathered_total(part, "rep"), as_sent(local_grad)),
    )
    large_new = (large_tables.astype(jnp.float32) - step_size * large_grad).astype(jnp.bfloat16)
    return (small_new, large_new)


def solution(mesh):
    placed = (
        P(("rep", "shard"), None),
        P(("rep", "shard"), None),
        P(("rep", "shard")),
        P(),
        P("shard", None, None),
        P(),
        P("shard", None, None),
        P("shard", None, None),
        P(),
        P(),
        P(),
    )
    return jax.shard_map(
        shards, mesh=mesh, in_specs=placed, out_specs=(P(), P("shard", None, None)), check_vma=False
    )
```

profile of v0, /device:TPU:1, one launch (start us, length us, event | category | flops | bytes accessed | tf_op | source)
XLA Modules:
  0.0 922.3 jit_solution(10983050159655116990)
XLA Ops:
  11.2 266.0 %gather_fusion = bf16[16384,128]{1,0:T(8,128)(2,1)} fusion(bf16[1,8192,128]{2,1,0:T(8,128)(2,1)} %param.15, s32[16384]{0:T(1024)S(1)} %bitcast.526), kind=kCustom, calls=%fused_computation | custom fusion | bytes 8519680 | tf_op jit(solution)/shard_map/vmap()/gather | solution.py:41
  277.2 6.3 convert_bitcast_fusion.2
  283.5 11.1 %all-to-all-start = ((bf16[1,64,128,128]{3,2,0,1:T(8,128)(2,1)}), bf16[1,64,128,128]{3,2,0,1:T(8,128)(2,1)S(1)}, u32[]{:S(2)}, u32[]{:S(2)}) async-start(bf16[1,64,128,128]{3,2,0,1:T(8,128)(2,1)} %convert_bitcast_fusion.2), calls=%async_computation | async-start | bytes 4194304 | tf_op jit(solution)/shard_map/all_to_all | solution.py:106
  294.9 8.1 convert_bitcast_fusion.3
  303.0 4.1 copy.345
  308.2 15.7 %all-to-all-done = bf16[1,64,128,128]{3,2,0,1:T(8,128)(2,1)S(1)} async-done(((bf16[1,64,128,128]{3,2,0,1:T(8,128)(2,1)}), bf16[1,64,128,128]{3,2,0,1:T(8,128)(2,1)S(1)}, u32[]{:S(2)}, u32[]{:S(2)}) %all-to-all-start) | async-done | bytes 2097184 | tf_op jit(solution)/shard_map/all_to_all | solution.py:106
  326.0 4.8 pad_maximum_fusion
  330.8 10.1 %copy.346 = bf16[256,97,128]{2,1,0:T(8,128)(2,1)} copy(bf16[256,97,128]{0,2,1:T(8,128)(2,1)} %pad_maximum_fusion) | data formatting | bytes 12713984 | tf_op jit(solution)/shard_map/concatenate | solution.py:117
  340.9 13.5 %fusion.60 = f32[256,97,97]{2,1,0:T(8,128)} fusion(bf16[256,97,128]{2,1,0:T(8,128)(2,1)} %copy.346), kind=kOutput, calls=%fused_computation.184 | convolution fusion | flops 616628224 | bytes 15991808 | tf_op jit(solution)/shard_map/bie,bje->bij/dot_general | solution.py:118
  528.4 14.2 %concatenate.14 = f32[256,4656]{1,0:T(8,128)} concatenate(f32[256,1]{1,0:T(8,128)S(1)} %bitcast.539, f32[256,2]{1,0:T(8,128)S(1)} %bitcast.540, f32[256,3]{1,0:T(8,128)S(1)} %bitcast.541, f32[256,4]{1,0:T(8,128)S(1)} %bitcast.542, f32[256,5]{1,0:T(8,128)S(1)} %bitcast.543, f32[256,6]{1,0:T(8,128)S(1)} %bitcast.544, f32[256,7]{1,0:T(8,128)S(1)} %bitcast.545, ...), dimensions={1} | concatenate | bytes 9535488 | tf_op jit(solution)/shard_map/concatenate | solution.py:46
  545.6 6.2 multiply_reduce_fusion
  628.2 15.5 %copy.443 = f32[256,97,97]{1,0,2:T(8,128)} copy(f32[256,97,97]{2,0,1:T(8,128)} %constant_dynamic-update-slice_fusion) | data formatting | bytes 19269632 | tf_op jit(solution)/shard_map/stack | solution.py:56
  643.7 12.3 %bitcast_add_fusion = bf16[256,97,97]{2,0,1:T(8,128)(2,1)} fusion(f32[256,97,97]{2,0,1:T(8,128)} %constant_dynamic-update-slice_fusion, f32[256,97,97]{1,0,2:T(8,128)} %copy.443), kind=kLoop, calls=%fused_computation.7 | loop fusion | flops 4817408 | bytes 24087040 | tf_op jit(solution)/shard_map/add | solution.py:130
  656.1 12.3 %fusion.11 = bf16[256,97,128]{2,1,0:T(8,128)(2,1)} fusion(bf16[256,97,128]{2,1,0:T(8,128)(2,1)S(1)} %bitcast.528, bf16[256,97,97]{2,0,1:T(8,128)(2,1)} %bitcast_add_fusion), kind=kOutput, calls=%fused_computation.20 | convolution fusion | flops 616628224 | bytes 17531392 | tf_op jit(solution)/shard_map/bij,bje->bie/dot_general | solution.py:131
  671.3 6.3 fusion
  677.7 5.1 slice.982
  682.8 5.9 convert_bitcast_fusion.1
  688.7 4.7 all-to-all-start.1
  694.2 33.1 %all-to-all-done.1 = bf16[64,1,128,128]{3,2,1,0:T(8,128)(2,1)S(1)} async-done(((bf16[64,1,128,128]{3,2,1,0:T(8,128)(2,1)}), bf16[64,1,128,128]{3,2,1,0:T(8,128)(2,1)S(1)}, u32[]{:S(2)}, u32[]{:S(2)}) %all-to-all-start.1) | async-done | bytes 2097184 | tf_op jit(solution)/shard_map/all_to_all | solution.py:146
  727.2 5.0 fusion.17
  732.2 90.0 %scatter_custom_fusion = f32[8192,128]{1,0:T(8,128)} fusion(s32[16384]{0:T(1024)S(1)} %broadcast_select_fusion, f32[16384,128]{1,0:T(8,128)} %bitcast.529, f32[]{:T(128)} %constant.16.clone.1), kind=kCustom, calls=%fused_computation.43 | custom fusion | flops 2097152 | bytes 4194816
  822.3 3.7 convert_element_type.266
  826.0 75.3 %all-reduce.98.cloned.1.call-done = f32[32,512,128]{2,1,0:T(8,128)} async-done(((f32[32,512,128]{2,1,0:T(8,128)}), f32[32,512,128]{2,1,0:T(8,128)}) %all-reduce.98.cloned.1.call-update) | async-done | bytes 8388624 | tf_op jit(solution)/shard_map/psum | solution.py:140
  901.3 8.0 subtract_convert_fusion
  (355 shorter events, 268.1 us)
Async XLA Ops:
  8.0 299.2 %copy-start = (s32[64,128]{1,0:T(8,128)S(1)}, s32[64,128]{1,0:T(8,128)}, u32[]{:S(2)}) copy-start(s32[64,128]{1,0:T(8,128)} %param.16) | copy-start | bytes 98308
  9.6 267.6 %copy-start.4 = (s32[64,128]{1,0:T(8,128)}, s32[64,128]{1,0:T(8,128)S(1)}, u32[]{:S(2)}) copy-start(s32[64,128]{1,0:T(8,128)S(1)} %get-tuple-element.7) | copy-start | bytes 98308
  277.2 17.7 %copy-start.11 = (s32[256,32]{0,1:T(8,128)S(1)}, s32[256,32]{0,1:T(8,128)}, u32[]{:S(2)}) copy-start(s32[256,32]{0,1:T(8,128)} %param.12) | copy-start | bytes 98308
  283.5 23.6 %copy-start.6 = (bf16[256,128]{1,0:T(8,128)(2,1)S(1)}, bf16[256,128]{1,0:T(8,128)(2,1)}, u32[]{:S(2)}) copy-start(bf16[256,128]{1,0:T(8,128)(2,1)} %param.11) | copy-start | bytes 196612
  283.5 40.4 %all-to-all-start = ((bf16[1,64,128,128]{3,2,0,1:T(8,128)(2,1)}), bf16[1,64,128,128]{3,2,0,1:T(8,128)(2,1)S(1)}, u32[]{:S(2)}, u32[]{:S(2)}) async-start(bf16[1,64,128,128]{3,2,0,1:T(8,128)(2,1)} %convert_bitcast_fusion.2), calls=%async_computation | async-start | bytes 4194304 | tf_op jit(solution)/shard_map/all_to_all | solution.py:106
  294.5 606.7 %all-reduce.98.cloned.1.call-start = ((), (), s32[]{:S(2)}) async-start(), calls=%async_computation.2 | async-start | bytes 16777216 | tf_op jit(solution)/shard_map/psum | solution.py:140
  524.4 21.1 %copy-start.13 = (f32[1024]{0:T(1024)S(1)}, f32[1024]{0:T(1024)}, u32[]{:S(2)}) copy-start(f32[1024]{0:T(1024)} %param.20) | copy-start | bytes 12292
  524.4 21.1 %copy-start.14 = (f32[1024]{0:T(1024)S(1)}, f32[1024]{0:T(1024)}, u32[]{:S(2)}) copy-start(f32[1024]{0:T(1024)} %param.21) | copy-start | bytes 12292
  542.6 9.2 slice-start.2
  545.5 6.2 copy-start.7
  545.5 6.3 slice-start.3
  545.6 6.3 slice-start.4
  554.9 9.9 %copy-start.10 = (pred[97]{0:T(512)(128)(4,1)S(1)}, pred[97]{0:T(512)(128)(4,1)}, u32[]{:S(2)}) copy-start(pred[97]{0:T(512)(128)(4,1)} %constant.17.clone.1) | copy-start | bytes 295
  628.2 27.8 %slice-start = ((s8[6815744]{0:T(1024)(128)(4,1)}), s8[2621440]{0:T(1024)(128)(4,1)S(1)}, s32[]{:S(2)}) async-start(s8[6815744]{0:T(1024)(128)(4,1)} %bitcast.527), calls=%async_computation.4 | async-start | bytes 5242880
  643.7 12.3 %slice-start.1 = ((s8[6815744]{0:T(1024)(128)(4,1)}), s8[4194304]{0:T(1024)(128)(4,1)S(1)}, s32[]{:S(2)}) async-start(s8[6815744]{0:T(1024)(128)(4,1)} %bitcast.527), calls=%async_computation.5 | async-start | bytes 8388608
  656.1 15.2 %copy-start.12 = (s32[256,32]{0,1:T(8,128)S(1)}, s32[256,32]{0,1:T(8,128)}, u32[]{:S(2)}) copy-start(s32[256,32]{0,1:T(8,128)} %param.12) | copy-start | bytes 98308
  677.6 15.8 %copy-start.3 = (s32[1,64,256]{2,1,0:T(8,128)S(1)}, s32[1,64,256]{2,1,0:T(8,128)}, u32[]{:S(2)}) copy-start(s32[1,64,256]{2,1,0:T(8,128)} %get-tuple-element.3) | copy-start | bytes 196612
  677.6 15.9 %copy-start.9 = (s32[2]{0:T(128)S(1)}, s32[2]{0:T(128)}, u32[]{:S(2)}) copy-start(s32[2]{0:T(128)} %constant.246) | copy-start | bytes 28
  677.6 16.2 %copy-start.8 = (s32[2]{0:T(128)S(1)}, s32[2]{0:T(128)}, u32[]{:S(2)}) copy-start(s32[2]{0:T(128)} %constant.249) | copy-start | bytes 28
  677.7 49.6 %copy-start.5 = (s32[64,128]{1,0:T(8,128)S(1)}, s32[64,128]{1,0:T(8,128)}, u32[]{:S(2)}) copy-start(s32[64,128]{1,0:T(8,128)} %copy-done.4) | copy-start | bytes 98308
  688.7 38.5 %all-to-all-start.1 = ((bf16[64,1,128,128]{3,2,1,0:T(8,128)(2,1)}), bf16[64,1,128,128]{3,2,1,0:T(8,128)(2,1)S(1)}, u32[]{:S(2)}, u32[]{:S(2)}) async-start(bf16[64,1,128,128]{3,2,1,0:T(8,128)(2,1)} %convert_bitcast_fusion.1), calls=%async_computation.1 | async-start | bytes 4194304 | tf_op jit(solution)/shard_map/all_to_all | solution.py:146
  693.4 215.9 %all-gather.3.cloned.1.call-start = ((), (), s32[]{:S(2)}) async-start(), calls=%async_computation.3 | async-start | bytes 6291456 | tf_op jit(solution)/shard_map/all_gather | solution.py:18
  826.0 86.7 %copy-start.2 = (bf16[1,8192,128]{2,1,0:T(8,128)(2,1)S(1)}, bf16[1,8192,128]{2,1,0:T(8,128)(2,1)}, u32[]{:S(2)}) copy-start(bf16[1,8192,128]{2,1,0:T(8,128)(2,1)} %param.15) | copy-start | bytes 6291460
  826.0 88.7 %copy-start.1 = (s32[64,128]{1,0:T(8,128)S(1)}, s32[64,128]{1,0:T(8,128)}, u32[]{:S(2)}) copy-start(s32[64,128]{1,0:T(8,128)} %param.16) | copy-start | bytes 98308
Sparse Core Ops, SparseCore 0:
  677.7 223.4 all-reduce.97
Sparse Core Ops, SparseCore 1:
  826.1 61.7 all-gather.2
where the time goes:
time: 933 us; the launch traced here: 922 us
  local copies, waits for them, and re-layouts  566 us (61%)
  other arithmetic  130 us (14%)
  waiting for transfers between devices  124 us (13%)
  matrix products  68.6 us (7%)
  between operations  17 us (2%)
  starting transfers between devices  16.1 us (2%)
    gather x2, local copies, waits for them, and re-layouts, take_rows(): return table_one[row_list]  266 us
    slice x96, local copies, waits for them, and re-layouts, lower_pairs(): pieces = [gram_matrix[:, index, :index] for index in range(1, vec_count)]  174 us
    unnamed x8, other arithmetic  91.3 us
    psum x1, waiting for transfers between devices, shards(): small_sum = lax.psum(small_local, ('rep', 'shard'))  75.3 us
    unnamed x137, local copies, waits for them, and re-layouts  63 us
    all_to_all x1, waiting for transfers between devices, shards(): lax.all_to_all(folded[:, None], 'shard', split_axis=0, concat_axis=1, til...  33.1 us
  transfers between devices with their start and end apart: 4, of which 3 were waited for; matrix products, arithmetic and copies ran while one was open for 14% of the time, Pallas kernels for 0%

commit v1 on v0

--- a/solution.py
+++ b/solution.py
@@ -137,7 +137,7 @@
         vec_grad[:, 1 : 1 + small_count],
         preferred_element_type=jnp.float32,
     )
-    small_sum = lax.psum(small_local, ("rep", "shard"))
+    small_sum = lax.psum(lax.psum(small_local, "shard"), "rep")
     small_new = (small_tables.astype(jnp.float32) - step_size * small_sum).astype(jnp.bfloat16)
     large_grad_part = vec_grad[:, 1 + small_count :]
     folded = jnp.einsum(

time: 933 us -> 1490 us (1.60)
  waiting for transfers between devices: 124 us -> 682 us
    psum x1 -> x2, waiting for transfers between devices: 75.3 us -> 634 us  [shards(): small_sum = lax.psum(lax.psum(small_local, 'shard'), 'rep')]
  transfers between devices with their start and end apart: 4 -> 5, of which waited for: 3 -> 4; matrix products, arithmetic and copies ran while one was open for 14% -> 9% of each run, Pallas kernels for 0% -> 0%
where the time goes in v1:
time: 1490 us; the launch traced here: 1480 us
  waiting for transfers between devices  682 us (46%)
  local copies, waits for them, and re-layouts  566 us (38%)
  other arithmetic  130 us (9%)
  matrix products  68.6 us (5%)
  between operations  17 us (1%)
  starting transfers between devices  16.2 us (1%)
    psum x2, waiting for transfers between devices, shards(): small_sum = lax.psum(lax.psum(small_local, 'shard'), 'rep')  634 us
    gather x2, local copies, waits for them, and re-layouts, take_rows(): return table_one[row_list]  266 us
    slice x96, local copies, waits for them, and re-layouts, lower_pairs(): pieces = [gram_matrix[:, index, :index] for index in range(1, vec_count)]  174 us
    unnamed x8, other arithmetic  91.3 us
    unnamed x137, local copies, waits for them, and re-layouts  63 us
    all_to_all x1, waiting for transfers between devices, shards(): lax.all_to_all(folded[:, None], 'shard', split_axis=0, concat_axis=1, til...  31.9 us
  transfers between devices with their start and end apart: 5, of which 4 were waited for; matrix products, arithmetic and copies ran while one was open for 9% of the time, Pallas kernels for 0%

profile of v1, /device:TPU:1, one launch (start us, length us, event | category | flops | bytes accessed | tf_op | source)
XLA Modules:
  0.0 1480.1 jit_solution(1628112282659745365)
XLA Ops:
  11.2 266.0 %gather_fusion = bf16[16384,128]{1,0:T(8,128)(2,1)} fusion(bf16[1,8192,128]{2,1,0:T(8,128)(2,1)} %param.15, s32[16384]{0:T(1024)S(1)} %bitcast.526), kind=kCustom, calls=%fused_computation | custom fusion | bytes 8519680 | tf_op jit(solution)/shard_map/vmap()/gather | solution.py:41
  277.2 6.3 convert_bitcast_fusion.2
  283.5 11.1 all-to-all-start
  294.9 8.1 convert_bitcast_fusion.3
  303.0 4.1 copy.345
  308.2 15.7 %all-to-all-done = bf16[1,64,128,128]{3,2,0,1:T(8,128)(2,1)S(1)} async-done(((bf16[1,64,128,128]{3,2,0,1:T(8,128)(2,1)}), bf16[1,64,128,128]{3,2,0,1:T(8,128)(2,1)S(1)}, u32[]{:S(2)}, u32[]{:S(2)}) %all-to-all-start) | async-done | bytes 2097184 | tf_op jit(solution)/shard_map/all_to_all | solution.py:106
  326.0 4.8 pad_maximum_fusion
  330.8 10.1 copy.346
  340.9 13.5 fusion.60
  528.4 14.2 concatenate.14
  545.6 6.2 multiply_reduce_fusion
  628.2 15.5 %copy.443 = f32[256,97,97]{1,0,2:T(8,128)} copy(f32[256,97,97]{2,0,1:T(8,128)} %constant_dynamic-update-slice_fusion) | data formatting | bytes 19269632 | tf_op jit(solution)/shard_map/stack | solution.py:56
  643.7 12.3 bitcast_add_fusion
  656.1 12.3 fusion.11
  671.3 6.3 fusion
  677.7 5.1 slice.982
  682.8 5.9 convert_bitcast_fusion.1
  688.7 4.7 all-to-all-start.1
  694.2 31.9 %all-to-all-done.1 = bf16[64,1,128,128]{3,2,1,0:T(8,128)(2,1)S(1)} async-done(((bf16[64,1,128,128]{3,2,1,0:T(8,128)(2,1)}), bf16[64,1,128,128]{3,2,1,0:T(8,128)(2,1)S(1)}, u32[]{:S(2)}, u32[]{:S(2)}) %all-to-all-start.1) | async-done | bytes 2097184 | tf_op jit(solution)/shard_map/all_to_all | solution.py:146
  726.1 5.0 fusion.17
  731.1 90.0 %scatter_custom_fusion = f32[8192,128]{1,0:T(8,128)} fusion(s32[16384]{0:T(1024)S(1)} %broadcast_select_fusion, f32[16384,128]{1,0:T(8,128)} %bitcast.529, f32[]{:T(128)} %constant.16.clone.1), kind=kCustom, calls=%fused_computation.43 | custom fusion | flops 2097152 | bytes 4194816
  825.0 433.2 %all-reduce.99.cloned.1.call-done = f32[32,512,128]{2,1,0:T(8,128)} async-done(((f32[32,512,128]{2,1,0:T(8,128)}), f32[32,512,128]{2,1,0:T(8,128)}) %all-reduce.99.cloned.1.call-update) | async-done | bytes 8388624 | tf_op jit(solution)/shard_map/psum | solution.py:140
  1263.7 200.8 %all-reduce.101.cloned.1.call-done = f32[32,512,128]{2,1,0:T(8,128)} async-done(((f32[32,512,128]{2,1,0:T(8,128)}), f32[32,512,128]{2,1,0:T(8,128)}) %all-reduce.101.cloned.1.call-update) | async-done | bytes 8388624 | tf_op jit(solution)/shard_map/psum | solution.py:140
  1464.5 8.0 subtract_convert_fusion
  (358 shorter events, 272.1 us)
Async XLA Ops:
  8.0 299.2 %copy-start = (s32[64,128]{1,0:T(8,128)S(1)}, s32[64,128]{1,0:T(8,128)}, u32[]{:S(2)}) copy-start(s32[64,128]{1,0:T(8,128)} %param.16) | copy-start | bytes 98308
  9.6 267.6 %copy-start.4 = (s32[64,128]{1,0:T(8,128)}, s32[64,128]{1,0:T(8,128)S(1)}, u32[]{:S(2)}) copy-start(s32[64,128]{1,0:T(8,128)S(1)} %get-tuple-element.7) | copy-start | bytes 98308
  277.2 17.7 %copy-start.11 = (s32[256,32]{0,1:T(8,128)S(1)}, s32[256,32]{0,1:T(8,128)}, u32[]{:S(2)}) copy-start(s32[256,32]{0,1:T(8,128)} %param.12) | copy-start | bytes 98308
  283.5 23.7 %copy-start.6 = (bf16[256,128]{1,0:T(8,128)(2,1)S(1)}, bf16[256,128]{1,0:T(8,128)(2,1)}, u32[]{:S(2)}) copy-start(bf16[256,128]{1,0:T(8,128)(2,1)} %param.11) | copy-start | bytes 196612
  283.5 40.4 %all-to-all-start = ((bf16[1,64,128,128]{3,2,0,1:T(8,128)(2,1)}), bf16[1,64,128,128]{3,2,0,1:T(8,128)(2,1)S(1)}, u32[]{:S(2)}, u32[]{:S(2)}) async-start(bf16[1,64,128,128]{3,2,0,1:T(8,128)(2,1)} %convert_bitcast_fusion.2), calls=%async_computation | async-start | bytes 4194304 | tf_op jit(solution)/shard_map/all_to_all | solution.py:106
  294.5 963.7 %all-reduce.99.cloned.1.call-start = ((), (), s32[]{:S(2)}) async-start(), calls=%async_computation.2 | async-start | bytes 16777216 | tf_op jit(solution)/shard_map/psum | solution.py:140
  524.4 21.1 %copy-start.13 = (f32[1024]{0:T(1024)S(1)}, f32[1024]{0:T(1024)}, u32[]{:S(2)}) copy-start(f32[1024]{0:T(1024)} %param.20) | copy-start | bytes 12292
  524.4 21.1 %copy-start.14 = (f32[1024]{0:T(1024)S(1)}, f32[1024]{0:T(1024)}, u32[]{:S(2)}) copy-start(f32[1024]{0:T(1024)} %param.21) | copy-start | bytes 12292
  542.6 9.2 slice-start.2
  545.5 6.3 slice-start.3
  545.6 6.3 slice-start.4
  554.9 9.9 copy-start.10
  628.2 27.8 %slice-start = ((s8[6815744]{0:T(1024)(128)(4,1)}), s8[2621440]{0:T(1024)(128)(4,1)S(1)}, s32[]{:S(2)}) async-start(s8[6815744]{0:T(1024)(128)(4,1)} %bitcast.527), calls=%async_computation.5 | async-start | bytes 5242880
  643.7 12.3 slice-start.1
  656.1 15.2 %copy-start.12 = (s32[256,32]{0,1:T(8,128)S(1)}, s32[256,32]{0,1:T(8,128)}, u32[]{:S(2)}) copy-start(s32[256,32]{0,1:T(8,128)} %param.12) | copy-start | bytes 98308
  677.6 15.8 %copy-start.3 = (s32[1,64,256]{2,1,0:T(8,128)S(1)}, s32[1,64,256]{2,1,0:T(8,128)}, u32[]{:S(2)}) copy-start(s32[1,64,256]{2,1,0:T(8,128)} %get-tuple-element.3) | copy-start | bytes 196612
  677.6 15.9 %copy-start.9 = (s32[2]{0:T(128)S(1)}, s32[2]{0:T(128)}, u32[]{:S(2)}) copy-start(s32[2]{0:T(128)} %constant.246) | copy-start | bytes 28
  677.6 16.2 %copy-start.8 = (s32[2]{0:T(128)S(1)}, s32[2]{0:T(128)}, u32[]{:S(2)}) copy-start(s32[2]{0:T(128)} %constant.249) | copy-start | bytes 28
  677.7 48.4 %copy-start.5 = (s32[64,128]{1,0:T(8,128)S(1)}, s32[64,128]{1,0:T(8,128)}, u32[]{:S(2)}) copy-start(s32[64,128]{1,0:T(8,128)} %copy-done.4) | copy-start | bytes 98308
  688.7 37.4 %all-to-all-start.1 = ((bf16[64,1,128,128]{3,2,1,0:T(8,128)(2,1)}), bf16[64,1,128,128]{3,2,1,0:T(8,128)(2,1)S(1)}, u32[]{:S(2)}, u32[]{:S(2)}) async-start(bf16[64,1,128,128]{3,2,1,0:T(8,128)(2,1)} %convert_bitcast_fusion.1), calls=%async_computation.1 | async-start | bytes 4194304 | tf_op jit(solution)/shard_map/all_to_all | solution.py:146
  693.4 564.9 %all-gather.3.cloned.1.call-start = ((), (), s32[]{:S(2)}) async-start(), calls=%async_computation.4 | async-start | bytes 6291456 | tf_op jit(solution)/shard_map/all_gather | solution.py:18
  821.1 440.6 %copy-start.2 = (bf16[1,8192,128]{2,1,0:T(8,128)(2,1)S(1)}, bf16[1,8192,128]{2,1,0:T(8,128)(2,1)}, u32[]{:S(2)}) copy-start(bf16[1,8192,128]{2,1,0:T(8,128)(2,1)} %param.15) | copy-start | bytes 6291460
  825.0 639.5 %all-reduce.101.cloned.1.call-start = ((), (), s32[]{:S(2)}) async-start(), calls=%async_computation.3 | async-start | bytes 16777216 | tf_op jit(solution)/shard_map/psum | solution.py:140
  1258.3 214.2 %copy-start.1 = (s32[64,128]{1,0:T(8,128)S(1)}, s32[64,128]{1,0:T(8,128)}, u32[]{:S(2)}) copy-start(s32[64,128]{1,0:T(8,128)} %param.16) | copy-start | bytes 98308
  (1 other events, 6.2 us)
Sparse Core Ops, SparseCore 0:
  677.7 580.4 all-reduce.98
Sparse Core Ops, SparseCore 1:
  825.1 67.9 all-gather.2
  1258.3 206.1 all-reduce.100
